TPU v7x, 32 devices: a whole 2x2x4 slice. The times are simulated.
32 devices in a mesh: grp: 4 (over y, core), rows: 8 (over z, x).
Axes of the slice: x: 2, y: 2, z: 4, core: 2. Of those that a mesh axis runs over, the one named last changes fastest.
Arguments:
- rhs: float32 [2048, 64, 128], P(('grp', 'rows')), may hold values from -6 to 6
- fine_diag: bfloat16 [2048, 64, 64], P(('grp', 'rows')), may hold values from -0.2 to 1.2
- fine_smoother: bfloat16 [2048, 64, 64], P(('grp', 'rows')), may hold values from -4 to 4
- fine_blocks: bfloat16 [2048, 7, 64, 64], P(('grp', 'rows')), may hold values from -0.1796875 to 0.1796875
- fine_cols: int32 [2048, 7], P(('grp', 'rows')), may hold values from 0 to 2047, as said below
- aggregate: int32 [2048], P(('grp', 'rows')), may hold values from 0 to 511, as said below
- coarse_diag: bfloat16 [512, 64, 64], P('rows'), may hold values from -0.8 to 4.8
- coarse_smoother: bfloat16 [512, 64, 64], P('rows'), may hold values from -1 to 1
- coarse_blocks: bfloat16 [512, 7, 64, 64], P('rows'), may hold values from -0.71875 to 0.71875
- coarse_cols: int32 [512, 7], P('rows'), may hold values from 0 to 511, as said below
Outputs:
- solution: float32 [2048, 64, 128], P(('grp', 'rows'))
Inputs may be any that keep to these rules, and one draw needn't show every extreme that they name: fine_cols row i names rows within 32 of i; the distance 32 is reached. coarse_cols row c names rows within 32 of c; the distance 32 is reached. `aggregate`: aggregate_i lies in [r * 64, (r + 1) * 64) with r = (i // 64) mod 8.
All inputs are finite; a program needn't handle non-finite values.
Results may differ from a plain program's by a relative error of at most 0.001.
The roundings to bfloat16 on the way count: a program that leaves them out, or rounds other values in their place, can miss the bound.
Values may be sent and summed in bfloat16 or wider, within the bound.
A program may use at most 128 MiB of HBM per device.

v0:
```python
import jax
import jax.numpy as jnp
from jax import lax
from jax.sharding import PartitionSpec as P

damping = 0.8


def extended_2(cells, sides, width):
    for axis, dim in sides:
        count = lax.axis_size(axis)
        ends = count - 1
        head = lax.slice_in_dim(cells, 0, width, axis=dim)
        tail = lax.slice_in_dim(cells, cells.shape[dim] - width, cells.shape[dim], axis=dim)
        cells = jnp.concatenate(
            [
                lax.ppermute(tail, axis, [(i, (i + 1) % count) for i in range(ends)]),
                cells,
                lax.ppermute(head, axis, [((i + 1) % count, i) for i in range(ends)]),
            ],
            axis=dim,
        )
    return cells


def block_product(blocks, vector):
    return jnp.einsum(
        "nab,nbk->nak", blocks, vector.astype(jnp.bfloat16), preferred_element_type=jnp.float32
    )


def nearby_product(off_blocks, columns, extended, first_row):
    nearby = jnp.take(extended, columns - first_row, axis=0)
    return jnp.einsum("njab,njbk->nak", off_blocks, nearby, preferred_element_type=jnp.float32)


def fine_operator(fine_diag, fine_blocks, fine_cols, vector):
    rounded_rows = vector.astype(jnp.bfloat16)
    height = vector.shape[0]
    margin = height // 2
    extended = extended_2(rounded_rows, ((("grp", "rows"), 0),), margin)
    first_row = lax.axis_index(("grp", "rows")) * height - margin
    return block_product(fine_diag, rounded_rows) + nearby_product(
        fine_blocks, fine_cols, extended, first_row
    )


def coarse_nearby(off_blocks, columns, rounded_full):
    height = rounded_full.shape[0]
    margin = height // 2
    extended = extended_2(rounded_full, (("rows", 0),), margin)
    first_row = lax.axis_index("rows") * height - margin
    return nearby_product(off_blocks, columns, extended, first_row)


def on_device(
    rhs,
    fine_diag,
    fine_smoother,
    fine_blocks,
    fine_cols,
    aggregate,
    coarse_diag,
    coarse_smoother,
    coarse_blocks,
    coarse_cols,
):
    first_iterate = damping * block_product(fine_smoother, rhs)
    first_residual = rhs - fine_operator(fine_diag, fine_blocks, fine_cols, first_iterate)
    second_iterate = first_iterate + damping * block_product(fine_smoother, first_residual)
    second_residual = rhs - fine_operator(fine_diag, fine_blocks, fine_cols, second_iterate)
    coarse_height = coarse_diag.shape[0]
    local_index = aggregate - lax.axis_index("rows") * coarse_height
    selector = (local_index[:, None] == jnp.arange(coarse_height, dtype=jnp.int32)[None, :]).astype(
        jnp.float32
    )
    partial_sum = jnp.einsum(
        "fc,fak->cak", selector, second_residual, precision=lax.Precision.HIGHEST
    )
    coarse_rhs = lax.psum(partial_sum, "grp")
    coarse_first = damping * block_product(coarse_smoother, coarse_rhs)
    rounded_first = coarse_first.astype(jnp.bfloat16)
    coarse_image = block_product(coarse_diag, rounded_first) + coarse_nearby(
        coarse_blocks, coarse_cols, rounded_first
    )
    coarse_second = coarse_first + damping * block_product(
        coarse_smoother, coarse_rhs - coarse_image
    )
    return second_iterate + jnp.take(coarse_second, local_index, axis=0)


def solution(mesh):
    in_specs = (
        P(("grp", "rows"), None, None),
        P(("grp", "rows"), None, None),
        P(("grp", "rows"), None, None),
        P(("grp", "rows"), None, None, None),
        P(("grp", "rows"), None),
        P(("grp", "rows")),
        P("rows", None, None),
        P("rows", None, None),
        P("rows", None, None, None),
        P("rows", None),
    )
    out_specs = P(("grp", "rows"), None, None)
    return jax.shard_map(
        on_device, mesh=mesh, in_specs=in_specs, out_specs=out_specs, check_vma=False
    )
```

profile of v0, /device:TPU:0, one launch (start us, length us, event | category | flops | bytes accessed | tf_op | source)
XLA Modules:
  0.0 246.3 jit_solution(17737860054501911996)
XLA Ops:
  6.5 0.0 copy-start
  6.5 0.0 all-reduce.2.cloned.1.call-start
  6.5 1.2 copy-done
  7.8 3.4 %multiply_convert_fusion.1 = (bf16[64,64,128]{2,1,0:T(8,128)(2,1)S(1)}, f32[64,64,128]{2,1,0:T(8,128)}) fusion(bf16[64,64,64]{2,1,0:T(8,128)(2,1)S(1)} %copy-done, f32[64,64,128]{2,1,0:T(8,128)} %param.12), kind=kOutput, calls=%fused_computation.33 | convolution fusion | flops 68681728 | bytes 5767168 | tf_op jit(solution)/shard_map/nab,nbk->nak/dot_general | solution.py:27
  11.1 1.0 fusion.39
  12.2 1.4 collective-permute-start.1
  13.6 6.3 %collective-permute-start = (bf16[32,64,128]{2,1,0:T(8,128)(2,1)}, bf16[32,64,128]{2,1,0:T(8,128)(2,1)}, u32[]{:S(2)}, u32[]{:S(2)}) collective-permute-start(bf16[32,64,128]{2,1,0:T(8,128)(2,1)} %get-tuple-element.16), channel_id=1, source_target_pairs={{0,1},{1,2},{2,3},{3,4},{4,5},{5,6},{6,7},{7,8},{8,9},{9,10},{10,1... | collective-permute-start | bytes 1572872 | tf_op jit(solution)/shard_map/ppermute | solution.py:17
  19.9 0.0 copy-done.11
  19.9 0.1 copy.18
  20.0 0.1 reshape.50
  20.1 0.1 copy.17
  20.3 0.0 copy-done.8
  20.3 1.8 fusion.43
  22.1 0.0 copy-done.4
  22.1 18.5 %collective-permute-done.1 = bf16[32,64,128]{2,1,0:T(8,128)(2,1)} collective-permute-done((bf16[32,64,128]{2,1,0:T(8,128)(2,1)}, bf16[32,64,128]{2,1,0:T(8,128)(2,1)}, u32[]{:S(2)}, u32[]{:S(2)}) %collective-permute-start.1) | collective-permute-done | bytes 524320 | tf_op jit(solution)/shard_map/ppermute | solution.py:19
  40.6 0.1 collective-permute-done
  40.7 1.8 pad_maximum_fusion
  42.4 13.3 %gather_fusion.1 = bf16[448,64,128]{2,1,0:T(8,128)(2,1)} fusion(bf16[128,64,128]{2,1,0:T(8,128)(2,1)S(1)} %pad_maximum_fusion, s32[1024]{0:T(1024)S(1)} %pad_clamp_fusion.2), kind=kCustom, calls=%fused_computation.clone | custom fusion | bytes 14681856 | tf_op jit(solution)/shard_map/jit(_take)/gather | solution.py:33
  55.8 10.1 %fusion.40 = (bf16[64,64,128]{2,1,0:T(8,128)(2,1)S(1)}, f32[64,64,128]{2,1,0:T(8,128)}) fusion(bf16[64,64,64]{2,1,0:T(8,128)(2,1)S(1)} %copy-done, f32[64,64,128]{2,1,0:T(8,128)} %param.12, f32[64,128,64]{1,2,0:T(8,128)} %fusion.43, bf16[64,7,64,64]{3,2,1,0:T(8,128)(2,1)} %param.15, bf16[64,7,64,128]{3,2,1,0:T(8,128)(2,1)} %bitcast.56, ...), kind=kOutput, calls=%fused_computation.61 | convolution fusion | flops 544210944 | bytes 20971968 | tf_op jit(solution)/shard_map/nab,nbk->nak/dot_general | solution.py:27
  65.9 0.1 fusion.38
  65.9 1.4 collective-permute-start.3
  67.4 5.2 %collective-permute-start.2 = (bf16[32,64,128]{2,1,0:T(8,128)(2,1)S(1)}, bf16[32,64,128]{2,1,0:T(8,128)(2,1)S(1)}, u32[]{:S(2)}, u32[]{:S(2)}) collective-permute-start(bf16[32,64,128]{2,1,0:T(8,128)(2,1)S(1)} %get-tuple-element.14), channel_id=1, source_target_pairs={{0,1},{1,2},{2,3},{3,4},{4,5},{5,6},{6,7},{7,8},{8,9},{9,10},{10,1... | collective-permute-start | bytes 1572872 | tf_op jit(solution)/shard_map/ppermute | solution.py:17
  72.6 0.0 copy-done.13
  72.6 0.0 copy-done.9
  72.6 1.8 fusion.44
  74.5 0.0 copy-done.5
  74.5 19.4 %collective-permute-done.3 = bf16[32,64,128]{2,1,0:T(8,128)(2,1)S(1)} collective-permute-done((bf16[32,64,128]{2,1,0:T(8,128)(2,1)S(1)}, bf16[32,64,128]{2,1,0:T(8,128)(2,1)S(1)}, u32[]{:S(2)}, u32[]{:S(2)}) %collective-permute-start.3) | collective-permute-done | bytes 524320 | tf_op jit(solution)/shard_map/ppermute | solution.py:19
  93.9 0.2 collective-permute-done.2
  94.1 1.5 pad_maximum_fusion.1
  95.5 13.3 %gather_fusion.2 = bf16[448,64,128]{2,1,0:T(8,128)(2,1)} fusion(bf16[128,64,128]{2,1,0:T(8,128)(2,1)S(1)} %pad_maximum_fusion.1, s32[1024]{0:T(1024)S(1)} %pad_clamp_fusion.2), kind=kCustom, calls=%fused_computation.1.clone | custom fusion | bytes 14681856 | tf_op jit(solution)/shard_map/jit(_take)/gather | solution.py:33
  108.9 9.2 %bitcast_subtract_fusion.1 = f32[64,64,128]{2,1,0:T(8,128)S(1)} fusion(f32[64,64,128]{2,1,0:T(8,128)} %param.12, f32[64,128,64]{1,2,0:T(8,128)} %fusion.44, bf16[64,7,64,64]{3,2,1,0:T(8,128)(2,1)} %param.15, bf16[64,7,64,128]{3,2,1,0:T(8,128)(2,1)} %bitcast.57, pred[64,7]{1,0:T(8,128)(4,1)S(1)} %copy.17), kind=kOutput, calls=%fused_computation.22 | convolution fusion | flops 474480640 | bytes 17301952 | tf_op jit(solution)/shard_map/njab,njbk->nak/dot_general | solution.py:34
  118.1 3.8 %fusion.14 = f32[64,64,128]{2,0,1:T(8,128)} fusion(f32[64,64,128]{2,1,0:T(8,128)S(1)} %bitcast_subtract_fusion.1, s32[64]{0:T(128)S(1)} %get-tuple-element.7), kind=kOutput, calls=%fused_computation.28 | convolution fusion | flops 402657280 | bytes 4194560 | tf_op jit(solution)/shard_map/fc,fak->cak/dot_general | solution.py:77
  121.9 0.0 all-reduce.2.cloned.1.call-update
  121.9 0.7 copy-done.12
  122.6 0.1 copy.24
  122.7 0.1 reshape.58
  122.8 51.9 %all-reduce.2.cloned.1.call-done = f32[64,64,128]{2,0,1:T(8,128)} async-done(((f32[64,64,128]{2,0,1:T(8,128)}), f32[64,64,128]{2,0,1:T(8,128)}) %all-reduce.2.cloned.1.call-update) | async-done | bytes 2097168 | tf_op jit(solution)/shard_map/psum | solution.py:80
  174.8 1.8 convert_element_type.29
  176.5 2.3 fusion.23
  178.8 0.3 fusion.27
  179.1 1.4 fusion.37
  180.5 1.5 collective-permute-start.5
  182.0 5.3 %collective-permute-start.4 = (bf16[32,64,128]{2,1,0:T(8,128)(2,1)}, bf16[32,64,128]{2,1,0:T(8,128)(2,1)}, u32[]{:S(2)}, u32[]{:S(2)}) collective-permute-start(bf16[32,64,128]{2,1,0:T(8,128)(2,1)} %get-tuple-element.12), channel_id=1, source_target_pairs={{0,1},{1,2},{2,3},{3,4},{4,5},{5,6},{6,7},{8,9},{9,10},{10,11},{11... | collective-permute-start | bytes 1572872 | tf_op jit(solution)/shard_map/ppermute | solution.py:17
  187.3 0.1 copy.23
  187.5 0.0 copy-done.2
  187.5 3.1 %fusion.28 = f32[64,128,64]{1,2,0:T(8,128)} fusion(bf16[64,64,64]{2,1,0:T(8,128)(2,1)} %param.18, f32[64,128,64]{1,2,0:T(8,128)S(1)} %fusion.23), kind=kOutput, calls=%fused_computation.40 | convolution fusion | flops 68157440 | bytes 4718592 | tf_op jit(solution)/shard_map/nab,nbk->nak/dot_general | solution.py:27
  190.5 5.6 %collective-permute-done.5 = bf16[32,64,128]{2,1,0:T(8,128)(2,1)} collective-permute-done((bf16[32,64,128]{2,1,0:T(8,128)(2,1)}, bf16[32,64,128]{2,1,0:T(8,128)(2,1)}, u32[]{:S(2)}, u32[]{:S(2)}) %collective-permute-start.5) | collective-permute-done | bytes 524320 | tf_op jit(solution)/shard_map/ppermute | solution.py:19
  196.1 11.1 %collective-permute-done.4 = bf16[32,64,128]{2,1,0:T(8,128)(2,1)} collective-permute-done((bf16[32,64,128]{2,1,0:T(8,128)(2,1)}, bf16[32,64,128]{2,1,0:T(8,128)(2,1)}, u32[]{:S(2)}, u32[]{:S(2)}) %collective-permute-start.4) | collective-permute-done | bytes 524320 | tf_op jit(solution)/shard_map/ppermute | solution.py:17
  207.2 1.4 pad_maximum_fusion.2
  208.7 13.3 %gather_fusion.3 = bf16[448,64,128]{2,1,0:T(8,128)(2,1)} fusion(bf16[128,64,128]{2,1,0:T(8,128)(2,1)S(1)} %pad_maximum_fusion.2, s32[1024]{0:T(1024)S(1)} %pad_clamp_fusion.1), kind=kCustom, calls=%fused_computation.2.clone | custom fusion | bytes 14681856 | tf_op jit(solution)/shard_map/jit(_take)/gather | solution.py:33
  222.0 0.0 copy-start.6
  222.0 0.0 copy-start.7
  222.1 6.8 %fusion = f32[64,128,64,1]{1,2,3,0:T(8,128)S(1)} fusion(bf16[64,7,64,64]{3,2,1,0:T(8,128)(2,1)} %param.20, bf16[64,7,64,128]{3,2,1,0:T(8,128)(2,1)} %bitcast.58, pred[64,7]{1,0:T(8,128)(4,1)S(1)} %copy.23), kind=kOutput, calls=%fused_computation.4 | convolution fusion | flops 473432064 | bytes 13107648 | tf_op jit(solution)/shard_map/njab,njbk->nak/dot_general | solution.py:34
  228.9 0.0 copy-done.6
  228.9 0.0 copy-done.7
  228.9 0.0 copy-start.3
  228.9 0.0 copy-start.10
  228.9 2.4 fusion.12
  231.3 0.0 copy-done.3
  231.3 0.0 copy-done.10
  231.3 2.6 %add_bitcast_fusion = f32[64,64,128]{2,1,0:T(8,128)} fusion(f32[64,128,64]{1,2,0:T(8,128)S(1)} %copy-done.3, bf16[64,64,64]{2,1,0:T(8,128)(2,1)S(1)} %copy-done.10, bf16[64,64,128]{2,0,1:T(8,128)(2,1)S(1)} %fusion.12), kind=kOutput, calls=%fused_computation.31 | convolution fusion | flops 68681728 | bytes 5767168 | tf_op jit(solution)/shard_map/nab,nbk->nak/dot_general | solution.py:27
  233.9 2.3 gather_fusion
  236.2 0.0 copy-start.1
  236.2 3.3 %select_add_fusion = f32[64,64,128]{2,1,0:T(8,128)} fusion(f32[64,64,128]{2,1,0:T(8,128)} %get-tuple-element.21, f32[64,64,128]{2,1,0:T(8,128)S(1)} %gather_fusion, pred[64]{0:T(512)(128)(4,1)S(1)} %get-tuple-element.6), kind=kLoop, calls=%fused_computation.30 | loop fusion | flops 1048576 | bytes 6291520 | tf_op jit(solution)/shard_map/add | solution.py:89
  (16 shorter events, 0.1 us)
Async XLA Ops:
  6.5 1.2 copy-start
  6.5 168.2 %all-reduce.2.cloned.1.call-start = ((), (), s32[]{:S(2)}) async-start(), calls=%async_computation | async-start | bytes 4194304 | tf_op jit(solution)/shard_map/psum | solution.py:80
  11.1 11.0 %copy-start.4 = (bf16[64,64,128]{2,1,0:T(8,128)(2,1)}, bf16[64,64,128]{2,1,0:T(8,128)(2,1)S(1)}, u32[]{:S(2)}) copy-start(bf16[64,64,128]{2,1,0:T(8,128)(2,1)S(1)} %get-tuple-element.18) | copy-start | bytes 3145732
  11.1 8.8 %copy-start.11 = (s32[64,7]{0,1:T(8,128)S(1)}, s32[64,7]{0,1:T(8,128)}, u32[]{:S(2)}) copy-start(s32[64,7]{0,1:T(8,128)} %param.16) | copy-start | bytes 5380
  11.1 9.1 %copy-start.8 = (bf16[64,64,64]{2,1,0:T(8,128)(2,1)S(1)}, bf16[64,64,64]{2,1,0:T(8,128)(2,1)}, u32[]{:S(2)}) copy-start(bf16[64,64,64]{2,1,0:T(8,128)(2,1)} %param.13) | copy-start | bytes 1572868
  12.2 28.5 %collective-permute-start.1 = (bf16[32,64,128]{2,1,0:T(8,128)(2,1)}, bf16[32,64,128]{2,1,0:T(8,128)(2,1)}, u32[]{:S(2)}, u32[]{:S(2)}) collective-permute-start(bf16[32,64,128]{2,1,0:T(8,128)(2,1)} %get-tuple-element.17), channel_id=1, source_target_pairs={{1,0},{2,1},{3,2},{4,3},{5,4},{6,5},{7,6},{8,7},{9,8},{10,9},{11,1... | collective-permute-start | bytes 1572872 | tf_op jit(solution)/shard_map/ppermute | solution.py:19
  13.6 27.1 %collective-permute-start = (bf16[32,64,128]{2,1,0:T(8,128)(2,1)}, bf16[32,64,128]{2,1,0:T(8,128)(2,1)}, u32[]{:S(2)}, u32[]{:S(2)}) collective-permute-start(bf16[32,64,128]{2,1,0:T(8,128)(2,1)} %get-tuple-element.16), channel_id=1, source_target_pairs={{0,1},{1,2},{2,3},{3,4},{4,5},{5,6},{6,7},{7,8},{8,9},{9,10},{10,1... | collective-permute-start | bytes 1572872 | tf_op jit(solution)/shard_map/ppermute | solution.py:17
  65.9 8.6 %copy-start.5 = (bf16[64,64,128]{2,1,0:T(8,128)(2,1)}, bf16[64,64,128]{2,1,0:T(8,128)(2,1)S(1)}, u32[]{:S(2)}) copy-start(bf16[64,64,128]{2,1,0:T(8,128)(2,1)S(1)} %get-tuple-element.20) | copy-start | bytes 3145732
  65.9 6.8 %copy-start.13 = (s32[64]{0:T(128)S(1)}, s32[64]{0:T(128)}, u32[]{:S(2)}) copy-start(s32[64]{0:T(128)} %param.17) | copy-start | bytes 772
  65.9 6.8 %copy-start.9 = (bf16[64,64,64]{2,1,0:T(8,128)(2,1)S(1)}, bf16[64,64,64]{2,1,0:T(8,128)(2,1)}, u32[]{:S(2)}) copy-start(bf16[64,64,64]{2,1,0:T(8,128)(2,1)} %param.13) | copy-start | bytes 1572868
  65.9 28.0 %collective-permute-start.3 = (bf16[32,64,128]{2,1,0:T(8,128)(2,1)S(1)}, bf16[32,64,128]{2,1,0:T(8,128)(2,1)S(1)}, u32[]{:S(2)}, u32[]{:S(2)}) collective-permute-start(bf16[32,64,128]{2,1,0:T(8,128)(2,1)S(1)} %get-tuple-element.15), channel_id=1, source_target_pairs={{1,0},{2,1},{3,2},{4,3},{5,4},{6,5},{7,6},{8,7},{9,8},{10,9},{11,1... | collective-permute-start | bytes 1572872 | tf_op jit(solution)/shard_map/ppermute | solution.py:19
  67.4 26.7 %collective-permute-start.2 = (bf16[32,64,128]{2,1,0:T(8,128)(2,1)S(1)}, bf16[32,64,128]{2,1,0:T(8,128)(2,1)S(1)}, u32[]{:S(2)}, u32[]{:S(2)}) collective-permute-start(bf16[32,64,128]{2,1,0:T(8,128)(2,1)S(1)} %get-tuple-element.14), channel_id=1, source_target_pairs={{0,1},{1,2},{2,3},{3,4},{4,5},{5,6},{6,7},{7,8},{8,9},{9,10},{10,1... | collective-permute-start | bytes 1572872 | tf_op jit(solution)/shard_map/ppermute | solution.py:17
  121.9 0.7 copy-start.12
  178.8 8.7 %copy-start.2 = (f32[64,128,64]{1,2,0:T(8,128)}, f32[64,128,64]{1,2,0:T(8,128)S(1)}, u32[]{:S(2)}) copy-start(f32[64,128,64]{1,2,0:T(8,128)S(1)} %fusion.23) | copy-start | bytes 6291460
  180.5 15.6 %collective-permute-start.5 = (bf16[32,64,128]{2,1,0:T(8,128)(2,1)}, bf16[32,64,128]{2,1,0:T(8,128)(2,1)}, u32[]{:S(2)}, u32[]{:S(2)}) collective-permute-start(bf16[32,64,128]{2,1,0:T(8,128)(2,1)} %get-tuple-element.13), channel_id=1, source_target_pairs={{1,0},{2,1},{3,2},{4,3},{5,4},{6,5},{7,6},{9,8},{10,9},{11,10},{12... | collective-permute-start | bytes 1572872 | tf_op jit(solution)/shard_map/ppermute | solution.py:19
  182.0 25.3 %collective-permute-start.4 = (bf16[32,64,128]{2,1,0:T(8,128)(2,1)}, bf16[32,64,128]{2,1,0:T(8,128)(2,1)}, u32[]{:S(2)}, u32[]{:S(2)}) collective-permute-start(bf16[32,64,128]{2,1,0:T(8,128)(2,1)} %get-tuple-element.12), channel_id=1, source_target_pairs={{0,1},{1,2},{2,3},{3,4},{4,5},{5,6},{6,7},{8,9},{9,10},{10,11},{11... | collective-permute-start | bytes 1572872 | tf_op jit(solution)/shard_map/ppermute | solution.py:17
  222.0 6.9 %copy-start.6 = (f32[64,64,128]{2,0,1:T(8,128)S(1)}, f32[64,64,128]{2,0,1:T(8,128)}, u32[]{:S(2)}) copy-start(f32[64,64,128]{2,0,1:T(8,128)} %all-reduce.2.cloned.1.call-done) | copy-start | bytes 6291460
  222.0 6.9 %copy-start.7 = (f32[64,128,64]{1,2,0:T(8,128)S(1)}, f32[64,128,64]{1,2,0:T(8,128)}, u32[]{:S(2)}) copy-start(f32[64,128,64]{1,2,0:T(8,128)} %fusion.28) | copy-start | bytes 6291460
  228.9 2.4 copy-start.3
  228.9 2.4 copy-start.10
  236.2 3.3 %copy-start.1 = (bf16[64,64,64]{2,1,0:T(8,128)(2,1)S(1)}, bf16[64,64,64]{2,1,0:T(8,128)(2,1)}, u32[]{:S(2)}) copy-start(bf16[64,64,64]{2,1,0:T(8,128)(2,1)} %param.14) | copy-start | bytes 1572868
Sparse Core Ops, SparseCore 0:
  122.0 52.6 all-reduce.1
where the time goes:
time: 247 us; the launch traced here: 246 us
  waiting for transfers between devices  107 us (43%)
  local copies, waits for them, and re-layouts  47.4 us (19%)
  matrix products  44.8 us (18%)
  starting transfers between devices  21.2 us (9%)
  between operations  13.7 us (6%)
  other arithmetic  12.4 us (5%)
    psum x1, waiting for transfers between devices, on_device(): coarse_rhs = lax.psum(partial_sum, 'grp')  51.9 us
    ppermute x3, waiting for transfers between devices, extended_2(): lax.ppermute(head, axis, [((i + 1) % count, i) for i in range(ends)])  43.5 us
    gather x3, local copies, waits for them, and re-layouts, nearby_product(): nearby = jnp.take(extended, columns - first_row, axis=0)  40 us
    dot_general x7, matrix products, block_product(): jnp.einsum('nab,nbk->nak', blocks, vector.astype(jnp.bfloat16), preferred...  25 us
    ppermute x3, starting transfers between devices, extended_2(): lax.ppermute(tail, axis, [(i, (i + 1) % count) for i in range(ends)])  16.9 us
    dot_general x2, matrix products, nearby_product(): jnp.einsum('njab,njbk->nak', off_blocks, nearby, preferred_element_type=j...  16 us
    ppermute x3, waiting for transfers between devices, extended_2(): lax.ppermute(tail, axis, [(i, (i + 1) % count) for i in range(ends)])  11.3 us
  transfers between devices with their start and end apart: 7, of which 7 were waited for; matrix products, arithmetic and copies ran while one was open for 3% of the time, Pallas kernels for 0%

commit v1 on v0

v1 whole, which is shorter than its diff:
```python
import functools

import jax
import jax.numpy as jnp
from jax import lax
from jax.experimental import pallas as pl
from jax.experimental.pallas import tpu as pltpu
from jax.sharding import PartitionSpec as P

MESH = pl.DeviceIdType.MESH
damping = 0.8
low = jnp.bfloat16
f32 = jnp.float32


def dot(a, b):
    return jnp.dot(a, b, preferred_element_type=f32)


def row_product(i, columns, offs, diag, extended, own):
    count = offs.shape[1]
    vectors = [extended[columns[i, k]] for k in range(count)] + [extended[own]]
    blocks = [offs[i, k] for k in range(count)] + [diag[i]]
    total = None
    for at in range(0, count + 1, 4):
        term = dot(
            jnp.concatenate(blocks[at : at + 4], axis=1),
            jnp.concatenate(vectors[at : at + 4], axis=0),
        )
        total = term if total is None else total + term
    return total


def kernel(
    groups, ranks,
    fine_cols, coarse_cols, aggregate, chain,
    rhs_hbm, diag_hbm, smoother_hbm, blocks_hbm, cdiag_hbm, csmoother_hbm, cblocks_hbm,
    out_hbm,
    rhs, diag, smoother, blocks, cdiag, csmoother, cblocks,
    ext1, ext2, landing, iterate, sums, partial, from_partner, chip_send, chip_recv, crhs, cfirst, cext, correction,
    load_sem, out_sem, halo_send, halo_recv, rs_send, rs_recv, rc_send, rc_recv,
    piece_send, piece_recv, ag_send, ag_recv, fwd_send, fwd_recv,
):
    g = lax.axis_index("grp")
    r = lax.axis_index("rows")
    height = rhs.shape[0]
    margin = height // 2
    cheight = partial.shape[0]
    piece = cheight // groups
    chips = groups // 2
    reach = groups // 2
    steps = 4
    chunk = margin // steps

    flat = g * ranks + r
    has_left = flat > 0
    has_right = flat < groups * ranks - 1
    left = ((flat - 1) // ranks, (flat + ranks - 1) % ranks)
    right = ((flat + 1) // ranks, (flat + 1) % ranks)
    core = g % 2
    chip = g // 2
    partner = (chip * 2 + 1 - core, r)

    def piece_of(group, rank):
        odd = rank % 2
        return odd * (groups - 1 - group) + (1 - odd) * group

    q = piece_of(g, r)
    linear = r * groups + q

    def holder(index):
        rank = index // groups
        return (piece_of(index % groups, rank), rank)

    def chip_peer(o):
        return (((chip + o) % chips) * 2 + core, r)

    shifts = [d for s in range(1, reach + 1) for d in (s, -s)]

    def exists(index):
        return jnp.logical_and(index >= 0, index < groups * ranks)

    def load(src, dst, at):
        return pltpu.make_async_copy(src, dst, load_sem.at[at])

    mine = pl.ds(q * piece, piece)
    first_loads = [load(rhs_hbm, rhs, 0), load(smoother_hbm, smoother, 1)]
    later_loads = [
        load(blocks_hbm, blocks, 2),
        load(diag_hbm, diag, 3),
        load(csmoother_hbm.at[mine], csmoother, 4),
        load(cdiag_hbm.at[mine], cdiag, 5),
        load(cblocks_hbm.at[mine], cblocks, 6),
    ]
    for c in first_loads:
        c.start()

    barrier = pltpu.get_barrier_semaphore()

    def greet(device):
        pl.semaphore_signal(barrier, inc=1, device_id=device, device_id_type=MESH)

    pl.when(has_left)(lambda: greet(left))
    pl.when(has_right)(lambda: greet(right))
    greet(partner)
    for o in range(1, chips):
        greet(chip_peer(o))
    met = 1 + chips - 1 + has_left.astype(jnp.int32) + has_right.astype(jnp.int32)
    for d in shifts:
        there = exists(linear + d)
        pl.when(there)(functools.partial(lambda d: greet(holder(linear + d)), d))
        met = met + there.astype(jnp.int32)
    pl.semaphore_wait(barrier, met)

    def remote(src, dst, send, recv, device):
        return pltpu.make_async_remote_copy(
            src_ref=src, dst_ref=dst, send_sem=send, recv_sem=recv, device_id=device, device_id_type=MESH
        )

    def to_right(ext, phase, j):
        src = ext.at[pl.ds(margin + height - (j + 1) * chunk, chunk)]
        at = pl.ds(margin - (j + 1) * chunk, chunk)
        dst = landing.at[0, at] if phase == 0 else ext.at[at]
        return remote(src, dst, halo_send.at[phase, 0, j], halo_recv.at[phase, 0, j], right)

    def to_left(ext, phase, j):
        src = ext.at[pl.ds(margin + j * chunk, chunk)]
        at = pl.ds(j * chunk, chunk)
        dst = landing.at[1, at] if phase == 0 else ext.at[pl.ds(margin + height + j * chunk, chunk)]
        return remote(src, dst, halo_send.at[phase, 1, j], halo_recv.at[phase, 1, j], left)

    def send_halo(ext, phase, j):
        pl.when(has_right)(lambda: to_right(ext, phase, j).start())
        pl.when(has_left)(lambda: to_left(ext, phase, j).start())

    def wait_halo(ext, phase, j):
        pl.when(has_left)(lambda: to_right(ext, phase, j).wait_recv())
        pl.when(has_right)(lambda: to_left(ext, phase, j).wait_recv())

    def wait_sent(ext, phase, j):
        pl.when(has_right)(lambda: to_right(ext, phase, j).wait_send())
        pl.when(has_left)(lambda: to_left(ext, phase, j).wait_send())

    def rows(start, count, body, unroll):
        def step(n, carry):
            body(start + n)
            return carry

        lax.fori_loop(0, count, step, 0, unroll=unroll)

    for c in first_loads:
        c.wait()

    def first(i):
        value = damping * dot(smoother[i], rhs[i].astype(low))
        iterate[i] = value
        ext1[margin + i] = value.astype(low)

    for j in range(steps):
        rows(height - (j + 1) * chunk, chunk, first, 4)
        rows(j * chunk, chunk, first, 4)
        send_halo(ext1, 0, j)
    for c in later_loads:
        c.start()
    later_loads[0].wait()
    later_loads[1].wait()

    def second(i):
        residual = rhs[i] - row_product(i, fine_cols, blocks, diag, ext1, margin + i)
        value = iterate[i] + damping * dot(smoother[i], residual.astype(low))
        iterate[i] = value
        ext2[margin + i] = value.astype(low)

    def place_low(i):
        ext1[i] = landing[0, i]

    def place_high(i):
        ext1[margin + height + i] = landing[1, i]

    for j in range(steps):
        wait_halo(ext1, 0, j)
        pl.when(has_left)(lambda: rows(margin - (j + 1) * chunk, chunk, place_low, 4))
        pl.when(has_right)(lambda: rows(j * chunk, chunk, place_high, 4))
        rows(margin - (j + 1) * chunk, chunk, second, 2)
        rows(margin + j * chunk, chunk, second, 2)
        send_halo(ext2, 1, steps - 1 - j)

    for j in reversed(range(steps)):
        wait_halo(ext2, 1, j)
    sums[height] = jnp.zeros(sums.shape[1:], f32)

    def third(n):
        i = height - 1 - n
        residual = rhs[i] - row_product(i, fine_cols, blocks, diag, ext2, margin + i)
        sums[i] = residual + sums[chain[i]]

    rows(0, height, third, 2)

    def gather(c):
        partial[c] = sums[chain[height + c]]

    rows(0, cheight, gather, 4)

    def slice_of(group):
        return pl.ds(piece_of(group, r) * piece, piece)

    def to_partner(o):
        src = partial.at[slice_of(((chip + o) % chips) * 2 + 1 - core)]
        return remote(src, from_partner.at[o], rs_send.at[o], rs_recv.at[o], partner)

    order = [*range(1, chips), 0]
    for o in order:
        to_partner(o).start()

    def across(o):
        return remote(chip_send.at[o], chip_recv.at[o], rc_send.at[o], rc_recv.at[o], chip_peer(o))

    for o in order:
        to_partner(o).wait_recv()
        start = piece_of(((chip + o) % chips) * 2 + core, r) * piece
        if o:
            def pack(n):
                chip_send[o, n] = (partial[start + n] + from_partner[o, n]).astype(low)

            rows(0, piece, pack, 2)
            across(o).start()
        else:
            def keep(n):
                crhs[n] = partial[start + n] + from_partner[o, n]

            rows(0, piece, keep, 2)
    for c in later_loads[2:]:
        c.wait()
    for o in range(1, chips):
        across(o).wait_recv()

    def coarse_first(n):
        total = crhs[n]
        for o in range(1, chips):
            total = total + chip_recv[o, n].astype(f32)
        crhs[n] = total
        value = damping * dot(csmoother[n], total.astype(low))
        cfirst[n] = value
        cext[reach * piece + n] = value.astype(low)

    rows(0, piece, coarse_first, 2)

    def to_shift(d):
        at = shifts.index(d)
        return remote(
            cext.at[pl.ds(reach * piece, piece)], cext.at[pl.ds((reach - d) * piece, piece)],
            piece_send.at[at], piece_recv.at[at], holder(linear + d),
        )

    for d in reversed(shifts):
        pl.when(exists(linear + d))(functools.partial(lambda d: to_shift(d).start(), d))
    for d in reversed(shifts):
        pl.when(exists(linear - d))(functools.partial(lambda d: to_shift(d).wait_recv(), d))

    def coarse_second(n):
        image = row_product(q * piece + n, coarse_cols, cblocks_view, cdiag_view, cext, reach * piece + n)
        value = cfirst[n] + damping * dot(csmoother[n], (crhs[n] - image).astype(low))
        correction[q * piece + n] = value.astype(low)

    class Shifted:
        def __init__(self, ref):
            self.ref, self.shape = ref, ref.shape

        def __getitem__(self, at):
            if isinstance(at, tuple):
                return self.ref[(at[0] - q * piece, *at[1:])]
            return self.ref[at - q * piece]

    cblocks_view, cdiag_view = Shifted(cblocks), Shifted(cdiag)
    rows(0, piece, coarse_second, 2)

    def piece_to(o):
        return remote(correction.at[mine], correction.at[mine], ag_send.at[o], ag_recv.at[o], chip_peer(o))

    def forward(o):
        at = slice_of(((chip + o) % chips) * 2 + core)
        return remote(correction.at[at], correction.at[at], fwd_send.at[o], fwd_recv.at[o], partner)

    for o in range(1, chips):
        piece_to(o).start()
    forward(0).start()
    for o in range(1, chips):
        piece_to(o).wait_recv()
        forward((chips - o) % chips).start()
    for o in range(chips):
        forward(o).wait_recv()

    part = height // 4

    def final(i):
        iterate[i] = iterate[i] + correction[aggregate[i]].astype(f32)

    def put(j):
        at = pl.ds(j * part, part)
        return pltpu.make_async_copy(iterate.at[at], out_hbm.at[at], out_sem.at[j])

    for j in range(4):
        rows(j * part, part, final, 4)
        put(j).start()

    for j in range(steps):
        wait_sent(ext1, 0, j)
        wait_sent(ext2, 1, j)
    for o in range(chips):
        to_partner(o).wait_send()
        forward(o).wait_send()
    for o in range(1, chips):
        across(o).wait_send()
        piece_to(o).wait_send()
    for d in shifts:
        pl.when(exists(linear + d))(functools.partial(lambda d: to_shift(d).wait_send(), d))
    for j in range(4):
        put(j).wait()


def chain_table(local_index, coarse_height):
    height = local_index.shape[0]
    row = jnp.arange(height, dtype=jnp.int32)
    wanted = jnp.concatenate([local_index, jnp.arange(coarse_height, dtype=jnp.int32)])
    after = jnp.concatenate([row, jnp.full((coarse_height,), -1, jnp.int32)])
    hit = (wanted[:, None] == local_index[None, :]) & (row[None, :] > after[:, None])
    return jnp.min(jnp.where(hit, row[None, :], height), axis=1)


def on_device(
    groups, ranks,
    rhs, fine_diag, fine_smoother, fine_blocks, fine_cols, aggregate,
    coarse_diag, coarse_smoother, coarse_blocks, coarse_cols,
):
    height, b, n = rhs.shape
    cheight = coarse_diag.shape[0]
    neighbours = fine_blocks.shape[1]
    piece = cheight // groups
    chips = groups // 2
    reach = groups // 2
    g, r = lax.axis_index("grp"), lax.axis_index("rows")
    odd = r % 2
    q = odd * (groups - 1 - g) + (1 - odd) * g
    fine_cols = fine_cols - ((g * ranks + r) * height - height // 2)
    coarse_cols = coarse_cols - (r * groups + q - reach) * piece
    aggregate = aggregate - r * cheight
    table = chain_table(aggregate, cheight)
    vmem = pltpu.VMEM
    dma = pltpu.SemaphoreType.DMA
    smem = pl.BlockSpec(memory_space=pltpu.SMEM)
    hbm = pl.BlockSpec(memory_space=pl.ANY)
    return pl.pallas_call(
        functools.partial(kernel, groups, ranks),
        out_shape=jax.ShapeDtypeStruct(rhs.shape, f32),
        in_specs=[smem] * 4 + [hbm] * 7,
        out_specs=hbm,
        scratch_shapes=[
            vmem((height, b, n), f32),
            vmem((height, b, b), low),
            vmem((height, b, b), low),
            vmem((height, neighbours, b, b), low),
            vmem((piece, b, b), low),
            vmem((piece, b, b), low),
            vmem((piece, neighbours, b, b), low),
            vmem((2 * height, b, n), low),
            vmem((2 * height, b, n), low),
            vmem((2, height // 2, b, n), low),
            vmem((height, b, n), f32),
            vmem((height + 1, b, n), f32),
            vmem((cheight, b, n), f32),
            vmem((chips, piece, b, n), f32),
            vmem((chips, piece, b, n), low),
            vmem((chips, piece, b, n), low),
            vmem((piece, b, n), f32),
            vmem((piece, b, n), f32),
            vmem(((2 * reach + 1) * piece, b, n), low),
            vmem((cheight, b, n), low),
            dma((7,)),
            dma((4,)),
            dma((2, 2, 4)),
            dma((2, 2, 4)),
            dma((chips,)),
            dma((chips,)),
            dma((chips,)),
            dma((chips,)),
            dma((2 * reach,)),
            dma((2 * reach,)),
            dma((chips,)),
            dma((chips,)),
            dma((chips,)),
            dma((chips,)),
        ],
        compiler_params=pltpu.CompilerParams(
            collective_id=0, has_side_effects=True, vmem_limit_bytes=60 * 1024 * 1024
        ),
        name="cycle",
    )(
        fine_cols, coarse_cols, aggregate, table,
        rhs, fine_diag, fine_smoother, fine_blocks, coarse_diag, coarse_smoother, coarse_blocks,
    )


def solution(mesh):
    fine = P(("grp", "rows"))
    return jax.shard_map(
        functools.partial(on_device, mesh.shape["grp"], mesh.shape["rows"]),
        mesh=mesh,
        in_specs=(fine,) * 6 + (P("rows"),) * 4,
        out_specs=fine,
        check_vma=False,
    )
```

time: 247 us -> 103 us (0.42)
  waiting for transfers between devices: 107 us -> 0 us
  Pallas kernels: 0 us -> 95.1 us
  matrix products: 44.8 us -> 0 us
  local copies, waits for them, and re-layouts: 47.4 us -> 4.72 us
  starting transfers between devices: 21.2 us -> 0 us
  between operations: 13.7 us -> 0.01 us
  other arithmetic: 12.4 us -> 2.58 us
    pallas_call x0 -> x1, Pallas kernels: none -> 95.1 us  [on_device(): pl.pallas_call(functools.partial(kernel, groups, ranks), out_shape=jax.Sh...]
    ppermute x6 -> x0, waiting for transfers between devices: 54.9 us -> none  [the longest x3 43.5 us: extended_2(): lax.ppermute(head, axis, [((i + 1) % count, i) for i in range(ends)])]
    psum x1 -> x0, waiting for transfers between devices: 51.9 us -> none  [on_device(): coarse_rhs = lax.psum(partial_sum, 'grp')]
    dot_general x10 -> x0, matrix products: 44.8 us -> none  [the longest x7 25 us: block_product(): jnp.einsum('nab,nbk->nak', blocks, vector.astype(jnp.bfloat16), preferred...]
    gather x4 -> x0, local copies, waits for them, and re-layouts: 42.3 us -> none  [the longest x3 40 us: nearby_product(): nearby = jnp.take(extended, columns - first_row, axis=0)]
    ppermute x6 -> x0, starting transfers between devices: 21.2 us -> none  [the longest x3 16.9 us: extended_2(): lax.ppermute(tail, axis, [(i, (i + 1) % count) for i in range(ends)])]
    concatenate x3 -> x1, other arithmetic: 4.66 us -> 0.08 us  [chain_table(): jnp.concatenate([local_index, jnp.arange(coarse_height, dtype=jnp.int32)])]
    convert_element_type x3 -> x0, other arithmetic: 4.45 us -> none  [the longest x2 4.14 us: block_product(): vector.astype(jnp.bfloat16)]
  transfers between devices with their start and end apart: 7 -> 0, of which waited for: 7 -> 0; matrix products, arithmetic and copies ran while one was open for 3% -> 0% of each run, Pallas kernels for 0% -> 0%
where the time goes in v1:
time: 103 us; the launch traced here: 102 us
  Pallas kernels  95.1 us (92%)
  local copies, waits for them, and re-layouts  4.72 us (5%)
  other arithmetic  2.58 us (3%)
    pallas_call x1, Pallas kernels, on_device(): pl.pallas_call(functools.partial(kernel, groups, ranks), out_shape=jax.Sh...  95.1 us
    unnamed x5, local copies, waits for them, and re-layouts  4.71 us

profile of v1, /device:TPU:0, one launch (start us, length us, event | category | flops | bytes accessed | tf_op | source)
XLA Modules:
  0.0 102.4 jit_solution(15101598931846358021)
XLA Ops:
  0.0 0.7 broadcast_subtract_fusion.2.aggregate
  0.7 0.0 copy-start
  0.7 0.1 pad_add_fusion
  0.7 1.2 %select_reduce_fusion.chain = s32[128]{0:T(128)} fusion(s32[128]{0:T(128)} %constant.40.clone.1, s32[128]{0:T(128)S(1)} %pad_add_fusion, s32[64]{0:T(128)S(1)} %broadcast_subtract_fusion.2.aggregate), kind=kLoop, calls=%fused_computation | loop fusion | flops 40832 | bytes 1792 | tf_op jit(solution)/shard_map/reduce_min | solution.py:327
  2.0 0.8 copy.15
  2.7 0.8 copy.17
  3.5 0.6 broadcast_subtract_fusion
  4.1 0.0 copy-done
  4.1 95.1 %cycle.1 = f32[64,64,128]{2,1,0:T(8,128)} custom-call(s32[64,7]{1,0:T(8,128)} %get-tuple-element.6.fine_cols, s32[64,7]{1,0:T(8,128)} %get-tuple-element.5.coarse_cols, s32[64]{0:T(128)} %copy-done, s32[128]{0:T(128)} %select_reduce_fusion.chain, f32[64,64,128]{2,1,0:T(8,128)} %rhs_hbm.1, bf16[64,64,64]{2,1,0:T(8,128)(2,1)} %diag_hbm.1, ...), custom_call_target="tpu_custom_call" | custom-call | tf_op jit(solution)/shard_map/cycle/pallas_call | solution.py:352
  99.3 3.2 %copy.20 = f32[64,64,128]{2,1,0:T(8,128)} copy(f32[64,64,128]{2,1,0:T(8,128)} %cycle.1) | data formatting | bytes 4194304
  (1 shorter events, 0.0 us)
Async XLA Ops:
  0.7 3.5 %copy-start = (s32[64]{0:T(128)}, s32[64]{0:T(128)S(1)}, u32[]{:S(2)}) copy-start(s32[64]{0:T(128)S(1)} %broadcast_subtract_fusion.2.aggregate) | copy-start | bytes 772

commit v2 on v1

v2 whole, which is shorter than its diff:
```python
import functools

import jax
import jax.numpy as jnp
import numpy as np
from jax import lax
from jax.experimental import pallas as pl
from jax.experimental.pallas import tpu as pltpu
from jax.sharding import PartitionSpec as P

MESH = pl.DeviceIdType.MESH
damping = 0.8
steps = 8
early = 1
parts = 4
low = jnp.bfloat16
f32 = jnp.float32


def dot(a, b):
    return jnp.dot(a, b, preferred_element_type=f32)


def row_product(i, columns, at, base, offs, diag, extended, own):
    count = offs.shape[1]
    last = extended.shape[0] - 1
    vectors = [extended[jnp.clip(columns[k, at] - base, 0, last)] for k in range(count)] + [extended[own]]
    blocks = [offs[i, k] for k in range(count)] + [diag[i]]
    total = None
    for p in range(0, count + 1, 4):
        term = dot(
            jnp.concatenate(blocks[p : p + 4], axis=1),
            jnp.concatenate(vectors[p : p + 4], axis=0),
        )
        total = term if total is None else total + term
    return total


def kernel(
    groups, ranks,
    fine_cols, coarse_cols, chain,
    rhs_hbm, diag_hbm, smoother_hbm, blocks_hbm, cdiag_hbm, csmoother_hbm, cblocks_hbm,
    iterate_hbm, correction_hbm,
    rhs, diag, smoother, blocks, cdiag, csmoother, cblocks,
    ext1, ext2, landing1, landing2, iterate, sums, partial, from_partner, chip_send, chip_recv, crhs, cfirst, cext, correction,
    load_sem, out_sem, halo_send, halo_recv, rs_send, rs_recv, rc_send, rc_recv,
    piece_send, piece_recv, ag_send, ag_recv, fwd_send, fwd_recv,
):
    g = lax.axis_index("grp")
    r = lax.axis_index("rows")
    height = rhs.shape[0]
    margin = height // 2
    cheight = partial.shape[0]
    piece = cheight // groups
    chips = groups // 2
    reach = groups // 2
    chunk = margin // steps
    share = piece // parts

    flat = g * ranks + r
    has_left = flat > 0
    has_right = flat < groups * ranks - 1
    left = ((flat - 1) // ranks, (flat + ranks - 1) % ranks)
    right = ((flat + 1) // ranks, (flat + 1) % ranks)
    core = g % 2
    chip = g // 2
    partner = (chip * 2 + 1 - core, r)

    def piece_of(group, rank):
        odd = rank % 2
        return odd * (groups - 1 - group) + (1 - odd) * group

    q = piece_of(g, r)
    linear = r * groups + q

    def holder(index):
        rank = index // groups
        return (piece_of(index % groups, rank), rank)

    def chip_peer(o):
        return (((chip + o) % chips) * 2 + core, r)

    shifts = [d for s in range(1, reach + 1) for d in (s, -s)]

    def exists(index):
        return jnp.logical_and(index >= 0, index < groups * ranks)

    def load(src, dst, at):
        return pltpu.make_async_copy(src, dst, load_sem.at[at])

    mine = pl.ds(q * piece, piece)
    first_loads = [load(rhs_hbm, rhs, 0), load(smoother_hbm, smoother, 1)]
    later_loads = [
        load(blocks_hbm, blocks, 2),
        load(diag_hbm, diag, 3),
        load(csmoother_hbm.at[mine], csmoother, 4),
        load(cdiag_hbm.at[mine], cdiag, 5),
        load(cblocks_hbm.at[mine], cblocks, 6),
    ]
    for c in first_loads:
        c.start()

    barrier = pltpu.get_barrier_semaphore()

    def greet(device):
        pl.semaphore_signal(barrier, inc=1, device_id=device, device_id_type=MESH)

    pl.when(has_left)(lambda: greet(left))
    pl.when(has_right)(lambda: greet(right))
    greet(partner)
    for o in range(1, chips):
        greet(chip_peer(o))
    met = 1 + chips - 1 + has_left.astype(jnp.int32) + has_right.astype(jnp.int32)
    for d in shifts:
        there = exists(linear + d)
        pl.when(there)(functools.partial(lambda d: greet(holder(linear + d)), d))
        met = met + there.astype(jnp.int32)
    pl.semaphore_wait(barrier, met)

    def remote(src, dst, send, recv, device):
        return pltpu.make_async_remote_copy(
            src_ref=src, dst_ref=dst, send_sem=send, recv_sem=recv, device_id=device, device_id_type=MESH
        )

    def to_right(ext, phase, j):
        src = ext.at[pl.ds(margin + height - (j + 1) * chunk, chunk)]
        at = pl.ds(margin - (j + 1) * chunk, chunk)
        dst = (landing1, landing2)[phase].at[0, at]
        return remote(src, dst, halo_send.at[phase, 0, j], halo_recv.at[phase, 0, j], right)

    def to_left(ext, phase, j):
        src = ext.at[pl.ds(margin + j * chunk, chunk)]
        at = pl.ds(j * chunk, chunk)
        dst = (landing1, landing2)[phase].at[1, at]
        return remote(src, dst, halo_send.at[phase, 1, j], halo_recv.at[phase, 1, j], left)

    def send_halo(ext, phase, j):
        pl.when(has_right)(lambda: to_right(ext, phase, j).start())
        pl.when(has_left)(lambda: to_left(ext, phase, j).start())

    def wait_halo(ext, phase, j):
        pl.when(has_left)(lambda: to_right(ext, phase, j).wait_recv())
        pl.when(has_right)(lambda: to_left(ext, phase, j).wait_recv())

    def wait_sent(ext, phase, j):
        pl.when(has_right)(lambda: to_right(ext, phase, j).wait_send())
        pl.when(has_left)(lambda: to_left(ext, phase, j).wait_send())

    def rows(start, count, body, unroll):
        def step(n, carry):
            body(start + n)
            return carry

        lax.fori_loop(0, count, step, 0, unroll=unroll)

    for c in first_loads:
        c.wait()

    def first(i):
        value = damping * dot(smoother[i], rhs[i].astype(low))
        iterate[i] = value
        ext1[margin + i] = value.astype(low)

    for j in range(steps):
        rows(height - (j + 1) * chunk, chunk, first, 4)
        rows(j * chunk, chunk, first, 4)
        send_halo(ext1, 0, j)
    for c in later_loads:
        c.start()
    later_loads[0].wait()
    later_loads[1].wait()

    def place(ext, landing, j):
        def place_low(i):
            ext[i] = landing[0, i]

        def place_high(i):
            ext[margin + height + i] = landing[1, i]

        pl.when(has_left)(lambda: rows(margin - (j + 1) * chunk, chunk, place_low, 4))
        pl.when(has_right)(lambda: rows(j * chunk, chunk, place_high, 4))

    base = flat * height - margin

    def second(i):
        residual = rhs[i] - row_product(i, fine_cols, i, base, blocks, diag, ext1, margin + i)
        value = iterate[i] + damping * dot(smoother[i], residual.astype(low))
        iterate[i] = value
        ext2[margin + i] = value.astype(low)

    for j in range(steps):
        wait_halo(ext1, 0, j)
        place(ext1, landing1, j)
        rows(margin - (j + 1) * chunk, chunk, second, 2)
        rows(margin + j * chunk, chunk, second, 2)
        if j < early:
            send_halo(ext2, 1, steps - 1 - j)
    for j in range(steps - early):
        send_halo(ext2, 1, j)
    keep_iterate = pltpu.make_async_copy(iterate, iterate_hbm, load_sem.at[7])
    keep_iterate.start()

    sums[0] = jnp.zeros(sums.shape[1:], f32)

    def third(shift):
        def body(i):
            residual = rhs[i] - row_product(i, fine_cols, i, base, blocks, diag, ext2, margin + i)
            sums[i + shift] = residual + sums[chain[i]]

        return body

    for j in reversed(range(steps - early, steps)):
        wait_halo(ext2, 1, j)
        place(ext2, landing2, j)
    for j in range(steps):
        if j < steps - early:
            wait_halo(ext2, 1, j)
            place(ext2, landing2, j)
        for n, start in enumerate((margin - (j + 1) * chunk, margin + j * chunk)):
            rows(start, chunk, third(1 + (2 * j + n) * chunk - start), 2)

    def gather(c):
        partial[c] = sums[chain[height + c]]

    rows(0, cheight, gather, 4)

    def slice_of(group, p):
        return pl.ds(piece_of(group, r) * piece + p * share, share)

    def to_partner(o, p):
        src = partial.at[slice_of(((chip + o) % chips) * 2 + 1 - core, p)]
        dst = from_partner.at[o, pl.ds(p * share, share)]
        return remote(src, dst, rs_send.at[o, p], rs_recv.at[o, p], partner)

    order = [*range(1, chips), 0]
    for o in order:
        for p in range(parts):
            to_partner(o, p).start()

    def across(o, p):
        at = pl.ds(p * share, share)
        return remote(chip_send.at[o, at], chip_recv.at[o, at], rc_send.at[o, p], rc_recv.at[o, p], chip_peer(o))

    for o in order:
        start = piece_of(((chip + o) % chips) * 2 + core, r) * piece

        def pack(n):
            chip_send[o, n] = (partial[start + n] + from_partner[o, n]).astype(low)

        def keep(n):
            crhs[n] = partial[start + n] + from_partner[o, n]

        for p in range(parts):
            to_partner(o, p).wait_recv()
            rows(p * share, share, pack if o else keep, 2)
            if o:
                across(o, p).start()
    for c in later_loads[2:]:
        c.wait()

    def coarse_first(n):
        total = crhs[n]
        for o in range(1, chips):
            total = total + chip_recv[o, n].astype(f32)
        crhs[n] = total
        value = damping * dot(csmoother[n], total.astype(low))
        cfirst[n] = value
        cext[reach * piece + n] = value.astype(low)

    def to_shift(d, p):
        at = shifts.index(d)
        return remote(
            cext.at[pl.ds(reach * piece + p * share, share)], cext.at[pl.ds((reach - d) * piece + p * share, share)],
            piece_send.at[at, p], piece_recv.at[at, p], holder(linear + d),
        )

    def each_part(method, d):
        for p in range(parts):
            getattr(to_shift(d, p), method)()

    for p in range(parts):
        for o in range(1, chips):
            across(o, p).wait_recv()
        rows(p * share, share, coarse_first, 2)
        for d in reversed(shifts):
            pl.when(exists(linear + d))(functools.partial(lambda d: to_shift(d, p).start(), d))
    for d in reversed(shifts):
        pl.when(exists(linear - d))(functools.partial(each_part, "wait_recv", d))

    cbase = (linear - reach) * piece

    def coarse_second(n):
        image = row_product(n, coarse_cols, q * piece + n, cbase, cblocks, cdiag, cext, reach * piece + n)
        value = cfirst[n] + damping * dot(csmoother[n], (crhs[n] - image).astype(low))
        correction[q * piece + n] = value.astype(low)

    def piece_to(o, p):
        at = slice_of(g, p)
        return remote(correction.at[at], correction.at[at], ag_send.at[o, p], ag_recv.at[o, p], chip_peer(o))

    def forward(o, p):
        at = slice_of(((chip + o) % chips) * 2 + core, p)
        return remote(correction.at[at], correction.at[at], fwd_send.at[o, p], fwd_recv.at[o, p], partner)

    def put(o, own, p):
        at = slice_of(((chip + o) % chips) * 2 + (core if own else 1 - core), p)
        return pltpu.make_async_copy(correction.at[at], correction_hbm.at[at], out_sem.at[o, own, p])

    for p in range(parts):
        rows(p * share, share, coarse_second, 2)
        for o in range(1, chips):
            piece_to(o, p).start()
        forward(0, p).start()
        put(0, 1, p).start()
    for o in range(1, chips):
        for p in range(parts):
            piece_to(o, p).wait_recv()
            forward(chips - o, p).start()
            put(chips - o, 1, p).start()
    for o in [0, *reversed(range(1, chips))]:
        for p in range(parts):
            forward(o, p).wait_recv()
            put(o, 0, p).start()

    for j in range(steps):
        wait_sent(ext1, 0, j)
        wait_sent(ext2, 1, j)
    for p in range(parts):
        for o in range(chips):
            to_partner(o, p).wait_send()
            forward(o, p).wait_send()
            put(o, 0, p).wait()
            put(o, 1, p).wait()
        for o in range(1, chips):
            across(o, p).wait_send()
            piece_to(o, p).wait_send()
    for d in shifts:
        pl.when(exists(linear + d))(functools.partial(each_part, "wait_send", d))
    keep_iterate.wait()


def add_kernel(cheight, aggregate, iterate, correction, out):
    count = out.shape[0]
    first = pl.program_id(0) * count
    start = lax.axis_index("rows") * cheight

    def step(n, carry):
        out[n] = iterate[n] + correction[aggregate[first + n] - start].astype(f32)
        return carry

    lax.fori_loop(0, count, step, 0, unroll=4)


def chain_table(aggregate, first_coarse, coarse_height, chunk):
    height = aggregate.shape[0]
    margin = height // 2
    row = np.arange(height)
    j = np.where(row < margin, margin - 1 - row, row - margin) // chunk
    start = np.where(row < margin, margin - (j + 1) * chunk, margin + j * chunk)
    slot = (1 + 2 * j * chunk + np.where(row < margin, 0, chunk) + row - start).astype(np.int32)
    limit = np.concatenate([slot, np.full(coarse_height, height + 1, np.int32)])
    wanted = jnp.concatenate([aggregate, first_coarse + jnp.arange(coarse_height, dtype=jnp.int32)])
    hit = (wanted[:, None] == aggregate[None, :]) & (slot[None, :] < limit[:, None])
    return jnp.max(jnp.where(hit, slot[None, :], 0), axis=1)


def on_device(
    groups, ranks,
    rhs, fine_diag, fine_smoother, fine_blocks, fine_cols, aggregate,
    coarse_diag, coarse_smoother, coarse_blocks, coarse_cols,
):
    height, b, n = rhs.shape
    cheight = coarse_diag.shape[0]
    neighbours = fine_blocks.shape[1]
    piece = cheight // groups
    chips = groups // 2
    reach = groups // 2
    chunk = height // 2 // steps
    table = chain_table(aggregate, lax.axis_index("rows") * cheight, cheight, chunk)
    vmem = pltpu.VMEM
    dma = pltpu.SemaphoreType.DMA
    smem = pl.BlockSpec(memory_space=pltpu.SMEM)
    hbm = pl.BlockSpec(memory_space=pl.ANY)
    iterate, correction = pl.pallas_call(
        functools.partial(kernel, groups, ranks),
        out_shape=(jax.ShapeDtypeStruct(rhs.shape, f32), jax.ShapeDtypeStruct((cheight, b, n), low)),
        in_specs=[smem] * 3 + [hbm] * 7,
        out_specs=(hbm, hbm),
        scratch_shapes=[
            vmem((height, b, n), f32),
            vmem((height, b, b), low),
            vmem((height, b, b), low),
            vmem((height, neighbours, b, b), low),
            vmem((piece, b, b), low),
            vmem((piece, b, b), low),
            vmem((piece, neighbours, b, b), low),
            vmem((2 * height, b, n), low),
            vmem((2 * height, b, n), low),
            vmem((2, height // 2, b, n), low),
            vmem((2, height // 2, b, n), low),
            vmem((height, b, n), f32),
            vmem((height + 1, b, n), f32),
            vmem((cheight, b, n), f32),
            vmem((chips, piece, b, n), f32),
            vmem((chips, piece, b, n), low),
            vmem((chips, piece, b, n), low),
            vmem((piece, b, n), f32),
            vmem((piece, b, n), f32),
            vmem(((2 * reach + 1) * piece, b, n), low),
            vmem((cheight, b, n), low),
            dma((8,)),
            dma((chips, 2, parts)),
            dma((2, 2, steps)),
            dma((2, 2, steps)),
            dma((chips, parts)),
            dma((chips, parts)),
            dma((chips, parts)),
            dma((chips, parts)),
            dma((2 * reach, parts)),
            dma((2 * reach, parts)),
            dma((chips, parts)),
            dma((chips, parts)),
            dma((chips, parts)),
            dma((chips, parts)),
        ],
        compiler_params=pltpu.CompilerParams(
            collective_id=0, has_side_effects=True, vmem_limit_bytes=60 * 1024 * 1024
        ),
        name="cycle",
    )(
        fine_cols.T, coarse_cols.T, table,
        rhs, fine_diag, fine_smoother, fine_blocks, coarse_diag, coarse_smoother, coarse_blocks,
    )
    share = height // 8
    return pl.pallas_call(
        functools.partial(add_kernel, cheight),
        out_shape=jax.ShapeDtypeStruct(rhs.shape, f32),
        grid=(height // share,),
        in_specs=[
            smem,
            pl.BlockSpec((share, b, n), lambda i: (i, 0, 0)),
            pl.BlockSpec((cheight, b, n), lambda i: (0, 0, 0)),
        ],
        out_specs=pl.BlockSpec((share, b, n), lambda i: (i, 0, 0)),
        name="add",
    )(aggregate, iterate, correction)


def solution(mesh):
    fine = P(("grp", "rows"))
    return jax.shard_map(
        functools.partial(on_device, mesh.shape["grp"], mesh.shape["rows"]),
        mesh=mesh,
        in_specs=(fine,) * 6 + (P("rows"),) * 4,
        out_specs=fine,
        check_vma=False,
    )
```

time: 103 us -> 94.6 us (0.918); the launches traced: 102 us -> 92.9 us
  local copies, waits for them, and re-layouts: 4.72 us -> 0 us
  Pallas kernels: 95.1 us -> 90.8 us
    unnamed x5 -> x0, local copies, waits for them, and re-layouts: 4.71 us -> none
    pallas_call x1 -> x2, Pallas kernels: 95.1 us -> 90.8 us  [the longest x1 84.7 us: on_device(): pl.pallas_call(functools.partial(kernel, groups, ranks), out_shape=(jax.S...]
    reduce_max x0 -> x1, other arithmetic: none -> 1.32 us  [chain_table(): return jnp.max(jnp.where(hit, slot[None, :], 0), axis=1)]
    sub x2 -> x0, other arithmetic: 1.28 us -> none  [the longest x1 0.66 us: on_device(): aggregate = aggregate - r * cheight]
    reduce_min x1 -> x0, other arithmetic: 1.23 us -> none  [chain_table(): return jnp.min(jnp.where(hit, row[None, :], height), axis=1)]
where the time goes in v2:
time: 94.6 us; the launch traced here: 92.9 us
  Pallas kernels  90.8 us (96%)
  other arithmetic  2.05 us (2%)
    pallas_call x1, Pallas kernels, on_device(): pl.pallas_call(functools.partial(kernel, groups, ranks), out_shape=(jax.S...  84.7 us
    pallas_call x1, Pallas kernels, on_device(): pl.pallas_call(functools.partial(add_kernel, cheight), out_shape=jax.Shap...  6.14 us

profile of v2, /device:TPU:0, one launch (start us, length us, event | category | flops | bytes accessed | tf_op | source)
XLA Modules:
  0.0 92.9 jit_solution(2253947956134982568)
XLA Ops:
  0.0 0.7 pad_add_fusion
  0.7 1.3 %select_reduce_fusion.chain = s32[128]{0:T(128)} fusion(pred[128,64]{0,1:T(32,128)(4,1)} %constant.14.clone, s32[64]{0:T(128)} %constant.16, s32[128]{0:T(128)S(1)} %pad_add_fusion, s32[64]{0:T(128)} %aggregate.1), kind=kLoop, calls=%fused_computation | loop fusion | flops 32640 | bytes 9728 | tf_op jit(solution)/shard_map/reduce_max | solution.py:364
  2.1 84.7 %cycle.1 = (f32[64,64,128]{2,1,0:T(8,128)}, bf16[64,64,128]{2,1,0:T(8,128)(2,1)}) custom-call(s32[7,64]{1,0:T(8,128)} %bitcast.2, s32[7,64]{1,0:T(8,128)} %bitcast.3, s32[128]{0:T(128)} %select_reduce_fusion.chain, f32[64,64,128]{2,1,0:T(8,128)} %rhs_hbm.1, bf16[64,64,64]{2,1,0:T(8,128)(2,1)} %diag_hbm.1, bf16[64,64,64]{2,1,0:T(8,128)(2,1)} %smoother_hbm.1, ...), custom_call_target="tpu_custom_call" | custom-call | tf_op jit(solution)/shard_map/cycle/pallas_call | solution.py:384
  86.8 6.1 %add.13 = f32[64,64,128]{2,1,0:T(8,128)} custom-call(s32[64]{0:T(128)} %aggregate.1, f32[64,64,128]{2,1,0:T(8,128)} %get-tuple-element.7.iterate, bf16[64,64,128]{2,1,0:T(8,128)(2,1)} %get-tuple-element.8.correction), custom_call_target="tpu_custom_call" | custom-call | tf_op jit(solution)/shard_map/add/pallas_call | solution.py:435
  (1 shorter events, 0.0 us)

commit v3 on v2

--- a/solution.py
+++ b/solution.py
@@ -2,7 +2,6 @@
 
 import jax
 import jax.numpy as jnp
-import numpy as np
 from jax import lax
 from jax.experimental import pallas as pl
 from jax.experimental.pallas import tpu as pltpu
@@ -38,11 +37,11 @@
 
 def kernel(
     groups, ranks,
-    fine_cols, coarse_cols, chain,
+    fine_cols, coarse_cols, aggregate,
     rhs_hbm, diag_hbm, smoother_hbm, blocks_hbm, cdiag_hbm, csmoother_hbm, cblocks_hbm,
     iterate_hbm, correction_hbm,
     rhs, diag, smoother, blocks, cdiag, csmoother, cblocks,
-    ext1, ext2, landing1, landing2, iterate, sums, partial, from_partner, chip_send, chip_recv, crhs, cfirst, cext, correction,
+    ext1, ext2, landing1, landing2, iterate, sums, partial, from_partner, chip_send, chip_recv, crhs, cfirst, cext, correction, chain,
     load_sem, out_sem, halo_send, halo_recv, rs_send, rs_recv, rc_send, rc_recv,
     piece_send, piece_recv, ag_send, ag_recv, fwd_send, fwd_recv,
 ):
@@ -167,8 +166,28 @@
         send_halo(ext1, 0, j)
     for c in later_loads:
         c.start()
-    later_loads[0].wait()
-    later_loads[1].wait()
+    starts = [at for j in range(steps) for at in (margin - (j + 1) * chunk, margin + j * chunk)]
+
+    def earlier(wanted, runs):
+        found = jnp.int32(0)
+        for n in range(runs):
+            for m in range(chunk):
+                found = jnp.where(aggregate[starts[n] + m] == wanted, 1 + n * chunk + m, found)
+        return found
+
+    def link_run(n):
+        def link(m):
+            wanted = aggregate[starts[n] + m]
+            found = earlier(wanted, n)
+            for k in range(chunk - 1):
+                same = jnp.logical_and(aggregate[starts[n] + k] == wanted, k < m)
+                found = jnp.where(same, 1 + n * chunk + k, found)
+            chain[starts[n] + m] = found
+
+        rows(0, chunk, link, 1)
+
+    def link_coarse(c):
+        chain[height + c] = earlier(r * cheight + c, len(starts))
 
     def place(ext, landing, j):
         def place_low(i):
@@ -179,6 +198,10 @@
 
         pl.when(has_left)(lambda: rows(margin - (j + 1) * chunk, chunk, place_low, 4))
         pl.when(has_right)(lambda: rows(j * chunk, chunk, place_high, 4))
+
+    rows(0, cheight // 2, link_coarse, 1)
+    later_loads[0].wait()
+    later_loads[1].wait()
 
     base = flat * height - margin
 
@@ -195,10 +218,15 @@
         rows(margin + j * chunk, chunk, second, 2)
         if j < early:
             send_halo(ext2, 1, steps - 1 - j)
+        if j < steps - 1:
+            link_run(2 * j)
+            link_run(2 * j + 1)
     for j in range(steps - early):
         send_halo(ext2, 1, j)
     keep_iterate = pltpu.make_async_copy(iterate, iterate_hbm, load_sem.at[7])
     keep_iterate.start()
+    link_run(2 * steps - 2)
+    link_run(2 * steps - 1)
 
     sums[0] = jnp.zeros(sums.shape[1:], f32)
 
@@ -218,6 +246,8 @@
             place(ext2, landing2, j)
         for n, start in enumerate((margin - (j + 1) * chunk, margin + j * chunk)):
             rows(start, chunk, third(1 + (2 * j + n) * chunk - start), 2)
+        if j < 4:
+            rows(cheight // 2 + j * (cheight // 8), cheight // 8, link_coarse, 1)
 
     def gather(c):
         partial[c] = sums[chain[height + c]]
@@ -339,29 +369,43 @@
     keep_iterate.wait()
 
 
-def add_kernel(cheight, aggregate, iterate, correction, out):
-    count = out.shape[0]
-    first = pl.program_id(0) * count
+def add_kernel(
+    cheight, aggregate, iterate_hbm, correction_hbm, out_hbm, iterate, correction, in_sem, correction_sem, out_sem
+):
+    share = iterate.shape[0] // 4
+    cshare = cheight // 4
     start = lax.axis_index("rows") * cheight
 
-    def step(n, carry):
-        out[n] = iterate[n] + correction[aggregate[first + n] - start].astype(f32)
-        return carry
-
-    lax.fori_loop(0, count, step, 0, unroll=4)
-
-
-def chain_table(aggregate, first_coarse, coarse_height, chunk):
-    height = aggregate.shape[0]
-    margin = height // 2
-    row = np.arange(height)
-    j = np.where(row < margin, margin - 1 - row, row - margin) // chunk
-    start = np.where(row < margin, margin - (j + 1) * chunk, margin + j * chunk)
-    slot = (1 + 2 * j * chunk + np.where(row < margin, 0, chunk) + row - start).astype(np.int32)
-    limit = np.concatenate([slot, np.full(coarse_height, height + 1, np.int32)])
-    wanted = jnp.concatenate([aggregate, first_coarse + jnp.arange(coarse_height, dtype=jnp.int32)])
-    hit = (wanted[:, None] == aggregate[None, :]) & (slot[None, :] < limit[:, None])
-    return jnp.max(jnp.where(hit, slot[None, :], 0), axis=1)
+    def fetch(j):
+        at = pl.ds(j * cshare, cshare)
+        return pltpu.make_async_copy(correction_hbm.at[at], correction.at[at], correction_sem.at[j])
+
+    def get(j):
+        at = pl.ds(j * share, share)
+        return pltpu.make_async_copy(iterate_hbm.at[at], iterate.at[at], in_sem.at[j])
+
+    def put(j):
+        at = pl.ds(j * share, share)
+        return pltpu.make_async_copy(iterate.at[at], out_hbm.at[at], out_sem.at[j])
+
+    for j in range(4):
+        fetch(j).start()
+    for j in range(4):
+        get(j).start()
+    for j in range(4):
+        fetch(j).wait()
+    for j in range(4):
+        get(j).wait()
+
+        def step(n, carry):
+            i = j * share + n
+            iterate[i] = iterate[i] + correction[aggregate[i] - start].astype(f32)
+            return carry
+
+        lax.fori_loop(0, share, step, 0, unroll=4)
+        put(j).start()
+    for j in range(4):
+        put(j).wait()
 
 
 def on_device(
@@ -375,8 +419,6 @@
     piece = cheight // groups
     chips = groups // 2
     reach = groups // 2
-    chunk = height // 2 // steps
-    table = chain_table(aggregate, lax.axis_index("rows") * cheight, cheight, chunk)
     vmem = pltpu.VMEM
     dma = pltpu.SemaphoreType.DMA
     smem = pl.BlockSpec(memory_space=pltpu.SMEM)
@@ -408,6 +450,7 @@
             vmem((piece, b, n), f32),
             vmem(((2 * reach + 1) * piece, b, n), low),
             vmem((cheight, b, n), low),
+            pltpu.SMEM((height + cheight,), jnp.int32),
             dma((8,)),
             dma((chips, 2, parts)),
             dma((2, 2, steps)),
@@ -428,20 +471,15 @@
         ),
         name="cycle",
     )(
-        fine_cols.T, coarse_cols.T, table,
+        fine_cols.T, coarse_cols.T, aggregate,
         rhs, fine_diag, fine_smoother, fine_blocks, coarse_diag, coarse_smoother, coarse_blocks,
     )
-    share = height // 8
     return pl.pallas_call(
         functools.partial(add_kernel, cheight),
         out_shape=jax.ShapeDtypeStruct(rhs.shape, f32),
-        grid=(height // share,),
-        in_specs=[
-            smem,
-            pl.BlockSpec((share, b, n), lambda i: (i, 0, 0)),
-            pl.BlockSpec((cheight, b, n), lambda i: (0, 0, 0)),
-        ],
-        out_specs=pl.BlockSpec((share, b, n), lambda i: (i, 0, 0)),
+        in_specs=[smem, hbm, hbm],
+        out_specs=hbm,
+        scratch_shapes=[vmem((height, b, n), f32), vmem((cheight, b, n), low), dma((4,)), dma((4,)), dma((4,))],
         name="add",
     )(aggregate, iterate, correction)
 

time: 94.6 us -> 91.6 us (0.968)
  other arithmetic: 2.05 us -> 0 us
    pallas_call x1, Pallas kernels: 6.14 us -> 3.8 us  [on_device(): pl.pallas_call(functools.partial(add_kernel, cheight), out_shape=jax.Shap...]
    pallas_call x1, Pallas kernels: 84.7 us -> 86.2 us  [on_device(): pl.pallas_call(functools.partial(kernel, groups, ranks), out_shape=(jax.S...]
    reduce_max x1 -> x0, other arithmetic: 1.32 us -> none  [chain_table(): return jnp.max(jnp.where(hit, slot[None, :], 0), axis=1)]
where the time goes in v3:
time: 91.6 us; the launch traced here: 90 us
  Pallas kernels  90 us (98%)
    pallas_call x1, Pallas kernels, on_device(): pl.pallas_call(functools.partial(kernel, groups, ranks), out_shape=(jax.S...  86.2 us
    pallas_call x1, Pallas kernels, on_device(): pl.pallas_call(functools.partial(add_kernel, cheight), out_shape=jax.Shap...  3.8 us

profile of v3, /device:TPU:0, one launch (start us, length us, event | category | flops | bytes accessed | tf_op | source)
XLA Modules:
  0.0 90.0 jit_solution(15751525644038181614)
XLA Ops:
  0.0 86.2 %cycle.1 = (f32[64,64,128]{2,1,0:T(8,128)}, bf16[64,64,128]{2,1,0:T(8,128)(2,1)}) custom-call(s32[7,64]{1,0:T(8,128)} %bitcast.2, s32[7,64]{1,0:T(8,128)} %bitcast.3, s32[64]{0:T(128)} %aggregate.3, f32[64,64,128]{2,1,0:T(8,128)} %rhs_hbm.1, bf16[64,64,64]{2,1,0:T(8,128)(2,1)} %diag_hbm.1, bf16[64,64,64]{2,1,0:T(8,128)(2,1)} %smoother_hbm.1, ...), custom_call_target="tpu_custom_call" | custom-call | tf_op jit(solution)/shard_map/cycle/pallas_call | solution.py:426
  86.2 3.8 %add.1 = f32[64,64,128]{2,1,0:T(8,128)} custom-call(s32[64]{0:T(128)} %aggregate.3, f32[64,64,128]{2,1,0:T(8,128)} %get-tuple-element.7.iterate_hbm, bf16[64,64,128]{2,1,0:T(8,128)(2,1)} %get-tuple-element.8.correction_hbm), custom_call_target="tpu_custom_call" | custom-call | tf_op jit(solution)/shard_map/add/pallas_call | solution.py:477

commit v4 on v3

--- a/solution.py
+++ b/solution.py
@@ -199,7 +199,7 @@
         pl.when(has_left)(lambda: rows(margin - (j + 1) * chunk, chunk, place_low, 4))
         pl.when(has_right)(lambda: rows(j * chunk, chunk, place_high, 4))
 
-    rows(0, cheight // 2, link_coarse, 1)
+    rows(0, cheight // 4, link_coarse, 1)
     later_loads[0].wait()
     later_loads[1].wait()
 
@@ -246,8 +246,8 @@
             place(ext2, landing2, j)
         for n, start in enumerate((margin - (j + 1) * chunk, margin + j * chunk)):
             rows(start, chunk, third(1 + (2 * j + n) * chunk - start), 2)
-        if j < 4:
-            rows(cheight // 2 + j * (cheight // 8), cheight // 8, link_coarse, 1)
+        if j < 6:
+            rows(cheight // 4 + j * (cheight // 8), cheight // 8, link_coarse, 1)
 
     def gather(c):
         partial[c] = sums[chain[height + c]]

time: 91.6 us -> 92.1 us (level)
  no operation moved by 1% of the time
where the time goes in v4:
time: 92.1 us; the launch traced here: 90.9 us
  Pallas kernels  90.9 us (99%)
    pallas_call x1, Pallas kernels, on_device(): pl.pallas_call(functools.partial(kernel, groups, ranks), out_shape=(jax.S...  87.1 us
    pallas_call x1, Pallas kernels, on_device(): pl.pallas_call(functools.partial(add_kernel, cheight), out_shape=jax.Shap...  3.8 us

profile of v4, /device:TPU:0, one launch (start us, length us, event | category | flops | bytes accessed | tf_op | source)
XLA Modules:
  0.0 90.9 jit_solution(13991963491723151619)
XLA Ops:
  0.0 87.1 %cycle.1 = (f32[64,64,128]{2,1,0:T(8,128)}, bf16[64,64,128]{2,1,0:T(8,128)(2,1)}) custom-call(s32[7,64]{1,0:T(8,128)} %bitcast.2, s32[7,64]{1,0:T(8,128)} %bitcast.3, s32[64]{0:T(128)} %aggregate.3, f32[64,64,128]{2,1,0:T(8,128)} %rhs_hbm.1, bf16[64,64,64]{2,1,0:T(8,128)(2,1)} %diag_hbm.1, bf16[64,64,64]{2,1,0:T(8,128)(2,1)} %smoother_hbm.1, ...), custom_call_target="tpu_custom_call" | custom-call | tf_op jit(solution)/shard_map/cycle/pallas_call | solution.py:426
  87.1 3.8 %add.1 = f32[64,64,128]{2,1,0:T(8,128)} custom-call(s32[64]{0:T(128)} %aggregate.3, f32[64,64,128]{2,1,0:T(8,128)} %get-tuple-element.7.iterate_hbm, bf16[64,64,128]{2,1,0:T(8,128)(2,1)} %get-tuple-element.8.correction_hbm), custom_call_target="tpu_custom_call" | custom-call | tf_op jit(solution)/shard_map/add/pallas_call | solution.py:477
